TPU v7x, 16 devices: a whole 2x2x2 slice. The times are simulated.
16 devices in a mesh: nodes: 16 (over z, y, x, core).
Axes of the slice: x: 2, y: 2, z: 2, core: 2. Of those that a mesh axis runs over, the one named last changes fastest.
Arguments:
- adjacency: bfloat16 [16384, 16384], P('nodes')
- features: bfloat16 [16384, 100], P('nodes')
- w_hidden: float32 [100, 256], replicated
- w_output: float32 [256, 47], replicated
- labels: int32 [16384], P('nodes')
- train_mask: int32 [16384], P('nodes')
- block_mask: int32 [16, 16], replicated
Outputs:
- output 1: float32 [], replicated
- output 2: float32 [100, 256], replicated
- output 3: float32 [256, 47], replicated
All inputs are finite; a program needn't handle non-finite values.
Results may differ from a plain program's by a relative error of at most 0.001.
Values are sent between devices in bfloat16 or wider.
A program may use at most 1 GiB of HBM per device.

v0:
```python
import jax
import jax.numpy as jnp
from jax import lax
from jax.sharding import PartitionSpec as P

AXIS_NAME = 'nodes'
ROW_CONTRACT = (((0,), (0,)), ((), ()))
LAST_CONTRACT = (((1,), (1,)), ((), ()))


def gather_masked(local_vals, mask_row):
    gathered = lax.all_gather(local_vals, AXIS_NAME, axis=0, tiled=False)
    gathered = gathered * mask_row.astype(local_vals.dtype)[:, None, None]
    return gathered.reshape(-1, local_vals.shape[-1])


def transpose_product_scatter(adj_rows, local_grad, mask_row):
    width = local_grad.shape[-1]
    contrib = lax.dot_general(adj_rows, local_grad, ROW_CONTRACT, preferred_element_type=jnp.float32)
    contrib = contrib.reshape(mask_row.shape[0], -1, width) * mask_row.astype(jnp.float32)[:, None, None]
    return lax.psum_scatter(contrib.reshape(-1, width), AXIS_NAME, scatter_dimension=0, tiled=True)


def device_step(adj_rows, feat_rows, w_hidden, w_output, labels, train_mask, block_mask):
    dev_index = lax.axis_index(AXIS_NAME)
    mask_row = lax.dynamic_index_in_dim(block_mask, dev_index, axis=0, keepdims=False)
    w_hidden_bf = w_hidden.astype(jnp.bfloat16)
    w_output_bf = w_output.astype(jnp.bfloat16)
    proj_one = jnp.dot(feat_rows, w_hidden_bf, preferred_element_type=jnp.float32).astype(jnp.bfloat16)
    agg_one = jnp.dot(adj_rows, gather_masked(proj_one, mask_row), preferred_element_type=jnp.float32)
    hidden = jnp.maximum(agg_one, 0.0).astype(jnp.bfloat16)
    proj_two = jnp.dot(hidden, w_output_bf, preferred_element_type=jnp.float32).astype(jnp.bfloat16)
    logits = jnp.dot(adj_rows, gather_masked(proj_two, mask_row), preferred_element_type=jnp.float32)
    label_weight = train_mask.astype(jnp.float32)
    log_norm = jax.nn.logsumexp(logits, axis=-1)
    one_hot = (labels[:, None] == jnp.arange(logits.shape[-1])[None, :]).astype(jnp.float32)
    picked = jnp.sum(logits * one_hot, axis=-1)
    totals = lax.psum(jnp.stack([jnp.sum(label_weight), jnp.sum(label_weight * (log_norm - picked))]), AXIS_NAME)
    label_count = totals[0]
    mean_loss = totals[1] / label_count
    probabilities = jnp.exp(logits - log_norm[:, None])
    grad_logits = ((probabilities - one_hot) * (label_weight / label_count)[:, None]).astype(jnp.bfloat16)
    grad_proj_two = transpose_product_scatter(adj_rows, grad_logits, mask_row).astype(jnp.bfloat16)
    grad_w_output = lax.psum(lax.dot_general(hidden, grad_proj_two, ROW_CONTRACT, preferred_element_type=jnp.float32), AXIS_NAME)
    grad_hidden = lax.dot_general(grad_proj_two, w_output_bf, LAST_CONTRACT, preferred_element_type=jnp.float32)
    grad_agg = jnp.where(agg_one > 0, grad_hidden, 0.0).astype(jnp.bfloat16)
    grad_proj_one = transpose_product_scatter(adj_rows, grad_agg, mask_row).astype(jnp.bfloat16)
    grad_w_hidden = lax.psum(lax.dot_general(feat_rows, grad_proj_one, ROW_CONTRACT, preferred_element_type=jnp.float32), AXIS_NAME)
    return mean_loss, grad_w_hidden, grad_w_output


def solution(mesh):
    row_spec = P(AXIS_NAME, None)
    vec_spec = P(AXIS_NAME)
    return jax.shard_map(device_step, mesh=mesh, in_specs=(row_spec, row_spec, P(), P(), vec_spec, vec_spec, P()), out_specs=(P(), P(), P()), check_vma=False)
```

profile of v0, /device:TPU:0, one launch (start us, length us, event | category | flops | bytes accessed | tf_op | source)
XLA Modules:
  0.0 512.1 jit_solution(5563643538842618410)
XLA Ops:
  7.2 0.9 copy-done
  8.1 2.1 convolution_convert_fusion
  10.3 0.7 convert_bitcast_fusion
  11.0 50.9 %all-gather.5.cloned.1.call-done = bf16[16384,256]{1,0:T(8,128)(2,1)} async-done(((bf16[1024,256]{1,0:T(8,128)(2,1)}), bf16[16384,256]{1,0:T(8,128)(2,1)}) %all-gather.5.cloned.1.call-update) | async-done | bytes 8388624 | tf_op jit(solution)/shard_map/all_gather | solution.py:12
  61.8 7.2 %broadcast_multiply_fusion = bf16[16,1024,256]{2,1,0:T(8,128)(2,1)} fusion(bf16[16,1024,256]{2,1,0:T(8,128)(2,1)} %bitcast.65, bf16[16]{0:T(256)(128)(2,1)S(1)} %get-tuple-element.9), kind=kLoop, calls=%fused_computation.4 | loop fusion | flops 4194304 | bytes 16777248 | tf_op jit(solution)/shard_map/mul | solution.py:13
  69.0 16.6 %fusion.33 = f32[256,1024]{1,0:T(8,128)S(1)} fusion(bf16[16384,256]{1,0:T(8,128)(2,1)} %bitcast.66, bf16[1024,16384]{1,0:T(8,128)(2,1)} %param.7), kind=kOutput, calls=%fused_computation.53 | convolution fusion | flops 8589934592 | bytes 42991616 | tf_op jit(solution)/shard_map/dot_general | solution.py:30
  85.7 0.9 convolution_convert_fusion.1
  86.7 27.3 %all-gather.7.cloned.1.call-done = bf16[16384,47]{0,1:T(8,128)(2,1)} async-done(((bf16[1024,47]{0,1:T(8,128)(2,1)}), bf16[16384,47]{0,1:T(8,128)(2,1)}) %all-gather.7.cloned.1.call-update) | async-done | bytes 1540112 | tf_op jit(solution)/shard_map/all_gather | solution.py:12
  114.0 2.3 copy.10
  116.6 0.9 copy.11
  117.6 15.2 %fusion.32 = (f32[1024]{0:T(1024)S(1)}, f32[47,1024]{1,0:T(8,128)S(1)}) fusion(bf16[16384,47]{0,1:T(8,128)(2,1)S(1)} %bitcast.67, bf16[1024,16384]{1,0:T(8,128)(2,1)} %param.7), kind=kOutput, calls=%fused_computation.52 | convolution fusion | flops 1577105408 | bytes 35291136 | tf_op jit(solution)/shard_map/dot_general | solution.py:33
  132.9 0.6 convert_reduce_fusion
  133.5 1.4 pad_maximum_fusion
  134.9 31.8 %psum.21 = f32[2]{0:T(128)S(1)} all-reduce(f32[2]{0:T(128)S(1)} %pad_maximum_fusion), channel_id=1, replica_groups=mesh['nodes'=16] {'nodes'}, use_global_device_ids=true, to_apply=%region_5.6 | all-reduce | flops 2 | bytes 16 | tf_op jit(solution)/shard_map/psum | solution.py:38
  166.7 0.6 fusion.31
  167.3 0.6 convert_divide_fusion
  168.0 15.4 %fusion.1 = f32[16384,47]{0,1:T(8,128)} fusion(bf16[1024,16384]{1,0:T(8,128)(2,1)} %param.7, f32[16384]{0:T(1024)S(1)} %bitcast.71, f32[47,1024]{1,0:T(8,128)S(1)} %get-tuple-element.13, f32[1024]{0:T(1024)S(1)} %convert_divide_fusion, f32[1024]{0:T(1024)S(1)} %get-tuple-element.7, s32[1024]{0:T(1024)S(1)} %copy-done.2), kind=kOutput, calls=%fused_computation.3 | convolution fusion | flops 1578117120 | bytes 36904960 | tf_op jit(solution)/shard_map/dot_general | solution.py:19
  183.7 55.2 %reduce-scatter.3.cloned.1.call-done = f32[1024,47]{0,1:T(8,128)} async-done(((f32[16384,47]{0,1:T(8,128)}), f32[1024,47]{0,1:T(8,128)}) %reduce-scatter.3.cloned.1.call-update) | async-done | bytes 192528 | tf_op jit(solution)/shard_map/reduce_scatter | solution.py:21
  238.9 18.6 %fusion = f32[16384,256]{0,1:T(8,128)} fusion(bf16[1024,16384]{1,0:T(8,128)(2,1)} %param.7, f32[16384]{0:T(1024)S(1)} %bitcast.72, f32[256,1024]{1,0:T(8,128)S(1)} %fusion.33, f32[1024,47]{0,1:T(8,128)} %reduce-scatter.3.cloned.1.call-done, f32[256,47]{0,1:T(8,128)S(1)} %copy-done.3), kind=kOutput, calls=%fused_computation.1 | convolution fusion | flops 8619617280 | bytes 51686400 | tf_op jit(solution)/shard_map/dot_general | solution.py:19
  258.9 176.0 %reduce-scatter.5.cloned.1.call-done = f32[1024,256]{0,1:T(8,128)} async-done(((f32[16384,256]{0,1:T(8,128)}), f32[1024,256]{0,1:T(8,128)}) %reduce-scatter.5.cloned.1.call-update) | async-done | bytes 1048592 | tf_op jit(solution)/shard_map/reduce_scatter | solution.py:21
  434.9 2.2 convolution_bitcast_fusion
  437.4 31.9 %psum.23 = f32[256,47]{0,1:T(8,128)} all-reduce(f32[256,47]{0,1:T(8,128)S(1)} %fusion.9), channel_id=1, replica_groups=mesh['nodes'=16] {'nodes'}, use_global_device_ids=true, to_apply=%region_9.10 | all-reduce | flops 12032 | bytes 96256 | tf_op jit(solution)/shard_map/psum | solution.py:44
  469.3 33.5 %all-reduce.2.cloned.1.call-done = f32[100,256]{1,0:T(8,128)} async-done(((f32[100,256]{1,0:T(8,128)}), f32[100,256]{1,0:T(8,128)}) %all-reduce.2.cloned.1.call-update) | async-done | bytes 102416 | tf_op jit(solution)/shard_map/psum | solution.py:48
  502.9 1.5 copy.14
  (26 shorter events, 1.3 us)
Async XLA Ops:
  7.2 0.9 copy-start
  7.2 54.7 %all-gather.5.cloned.1.call-start = ((), (), s32[]{:S(2)}) async-start(), calls=%async_computation.5 | async-start | bytes 8912896 | tf_op jit(solution)/shard_map/all_gather | solution.py:12
  10.2 103.8 %all-gather.7.cloned.1.call-start = ((), (), s32[]{:S(2)}) async-start(), calls=%async_computation.6 | async-start | bytes 1671168 | tf_op jit(solution)/shard_map/all_gather | solution.py:12
  69.0 16.6 %copy-start.3 = (f32[256,47]{0,1:T(8,128)S(1)}, f32[256,47]{0,1:T(8,128)}, u32[]{:S(2)}) copy-start(f32[256,47]{0,1:T(8,128)} %param.10) | copy-start | bytes 144388
  86.5 152.3 %reduce-scatter.3.cloned.1.call-start = ((), (), s32[]{:S(2)}) async-start(), calls=%async_computation.2 | async-start | bytes 3342336 | tf_op jit(solution)/shard_map/reduce_scatter | solution.py:21
  117.6 15.2 %copy-start.2 = (s32[1024]{0:T(1024)S(1)}, s32[1024]{0:T(1024)}, u32[]{:S(2)}) copy-start(s32[1024]{0:T(1024)} %param.11) | copy-start | bytes 12292
  117.6 15.3 %copy-start.4 = (s32[1024]{0:T(1024)S(1)}, s32[1024]{0:T(1024)}, u32[]{:S(2)}) copy-start(s32[1024]{0:T(1024)} %param.12) | copy-start | bytes 12292
  183.4 251.5 %reduce-scatter.5.cloned.1.call-start = ((), (), s32[]{:S(2)}) async-start(), calls=%async_computation.3 | async-start | bytes 17825792 | tf_op jit(solution)/shard_map/reduce_scatter | solution.py:21
  257.4 179.7 %copy-start.1 = (f32[1024,47]{0,1:T(8,128)S(1)}, f32[1024,47]{0,1:T(8,128)}, u32[]{:S(2)}) copy-start(f32[1024,47]{0,1:T(8,128)} %reduce-scatter.3.cloned.1.call-done) | copy-start | bytes 577540
  257.5 245.4 %all-reduce.2.cloned.1.call-start = ((), (), s32[]{:S(2)}) async-start(), calls=%async_computation.4 | async-start | bytes 212992 | tf_op jit(solution)/shard_map/psum | solution.py:48
Sparse Core Ops, SparseCore 0:
  10.3 51.4 all-gather.4
  86.7 27.2 all-gather.6
  183.6 55.2 reduce-scatter.2
  257.6 177.2 reduce-scatter.4
  439.6 63.2 all-reduce.1
where the time goes:
time: 513 us; the launch traced here: 512 us
  waiting for transfers between devices  343 us (67%)
  matrix products  71.2 us (14%)
  blocking collectives  63.7 us (12%)
  between operations  16.4 us (3%)
  other arithmetic  10.8 us (2%)
  local copies, waits for them, and re-layouts  6.52 us (1%)
    reduce_scatter x2, waiting for transfers between devices, transpose_product_scatter(): lax.psum_scatter(contrib.reshape(-1, width), AXIS_NAME, scatter_dimension...  231 us
    all_gather x2, waiting for transfers between devices, gather_masked(): gathered = lax.all_gather(local_vals, AXIS_NAME, axis=0, tiled=False)  78.2 us
    dot_general x2, matrix products, transpose_product_scatter(): lax.dot_general(adj_rows, local_grad, ROW_CONTRACT, preferred_element_typ...  34 us
    psum x1, waiting for transfers between devices, device_step(): lax.psum(lax.dot_general(feat_rows, grad_proj_one, ROW_CONTRACT, preferre...  33.5 us
    psum x1, blocking collectives, device_step(): lax.psum(lax.dot_general(hidden, grad_proj_two, ROW_CONTRACT, preferred_e...  31.9 us
    psum x1, blocking collectives, device_step(): lax.psum(jnp.stack([jnp.sum(label_weight), jnp.sum(label_weight * (log_no...  31.8 us
    dot_general x1, matrix products, device_step(): jnp.dot(adj_rows, gather_masked(proj_one, mask_row), preferred_element_ty...  16.6 us
    dot_general x1, matrix products, device_step(): jnp.dot(adj_rows, gather_masked(proj_two, mask_row), preferred_element_ty...  15.2 us
  transfers between devices with their start and end apart: 5, of which 5 were waited for; matrix products, arithmetic and copies ran while one was open for 0% of the time, Pallas kernels for 0%

commit v1 on v0

v1 whole, which is shorter than its diff:
```python
import functools

import jax
import jax.numpy as jnp
from jax import lax
from jax.experimental import pallas as pl
from jax.experimental.pallas import tpu as pltpu
from jax.sharding import PartitionSpec as P

AXIS = 'nodes'
MESH = pl.DeviceIdType.MESH
F32, BF16 = jnp.float32, jnp.bfloat16
LAST = (((1,), (1,)), ((), ()))
NB, BR, FI, HID, NC, CP = 16, 1024, 100, 256, 47, 48
X, Y, Z = 1, 2, 4
DIMS = (X, Y, Z)
NEXT = {X: Y, Y: Z, Z: X}
PREV = {Y: X, Z: Y, X: Z}
XYZ = X + Y + Z
LOSS_LANE = 64

ORDER = [(0, 0), (0, 1)]
for group in ((X, Y, Z), (X + Y, Y + Z, Z + X), (XYZ,)):
    ORDER += [(q, 0) for q in group] + [(q, 1) for q in group]
SLOT = {qc: i for i, qc in enumerate(ORDER)}

AG_COPIES, RS_COPIES = 17, 29
AG_X, AG_Y = 0, AG_COPIES
RS_D2, RS_D1 = 2 * AG_COPIES, 2 * AG_COPIES + RS_COPIES
AR = 2 * AG_COPIES + 2 * RS_COPIES
N_SEM = AR + 30


def peer(me, mask):
    out = me
    for k in range(4):
        if mask >> k & 1:
            out = out + (1 - 2 * (me // (1 << k) % 2)) * (1 << k)
    return out


def kernel(a_hbm, x_hbm, wh_ref, wo_ref, lab_ref, tm_ref,
           loss_ref, gwh_ref, gwo_ref,
           a_v, xg, yg, z1, hid, pos, z2, r2, ra2, rb2, rc2, r1, ra1, rb1, rc1, stage, wop,
           fsrc, frecv, fsum, fall, a_sem, x_sem, send_sem, recv_sem):
    me = lax.axis_index(AXIS)
    devs = {m: peer(me, m) for m in range(16)}

    def rcopy(src, dst, k, mask):
        return pltpu.make_async_remote_copy(
            src_ref=src, dst_ref=dst, send_sem=send_sem.at[k], recv_sem=recv_sem.at[k],
            device_id=(devs[mask],), device_id_type=MESH)

    a_copies = []
    for s, (q, c) in enumerate(ORDER):
        col = pl.multiple_of(devs[2 * q + c] * BR, BR)
        a_copies.append(pltpu.make_async_copy(a_hbm.at[:, pl.ds(col, BR)], a_v.at[s], a_sem.at[s]))
    x_copy = pltpu.make_async_copy(x_hbm, xg.at[0], x_sem)
    x_copy.start()
    for cp in a_copies:
        cp.start()

    barrier = pltpu.get_barrier_semaphore()
    for m in range(1, 16):
        pl.semaphore_signal(barrier, inc=1, device_id=(devs[m],), device_id_type=MESH)
    wop[...] = jnp.zeros_like(wop)
    wop[:, :NC] = wo_ref[...].astype(BF16)
    fsrc[...] = jnp.zeros_like(fsrc)
    z2[...] = jnp.zeros_like(z2)
    z1[...] = jnp.zeros_like(z1)
    pl.semaphore_wait(barrier, 15)
    x_copy.wait()

    sent = []

    def start(cp):
        cp.start()
        sent.append(cp)
        return cp

    def gather(base, g, pieces, work):
        def core_fwd(q):
            return start(rcopy(g.at[SLOT[q, 0]], g.at[SLOT[q, 1]], base + 9 + q, 1))

        one = {d: start(rcopy(g.at[0], g.at[SLOT[d, 0]], base + i, 2 * d)) for i, d in enumerate(DIMS)}
        half = {0: core_fwd(0)}
        work(0, 1)
        half[0].wait_recv()
        work(1, 2)
        two, three = {}, {}
        for d in DIMS:
            one[d].wait_recv()
        for i, d in enumerate(DIMS):
            e = NEXT[d]
            two[d] = start(rcopy(g.at[SLOT[e, 0]], g.at[SLOT[d + e, 0]], base + 3 + i, 2 * d))
        for d in DIMS:
            half[d] = core_fwd(d)
        work(2, 5)
        for d in DIMS:
            half[d].wait_recv()
        work(5, 8)
        for d in DIMS:
            two[d].wait_recv()
        for i, d in enumerate(DIMS):
            rows = pl.ds(*pieces[i])
            three[d] = start(rcopy(g.at[SLOT[XYZ - d, 0], rows], g.at[SLOT[XYZ, 0], rows], base + 6 + i, 2 * d))
        for d in DIMS:
            half[XYZ - d] = core_fwd(XYZ - d)
        work(8, 11)
        for d in DIMS:
            half[XYZ - d].wait_recv()
        work(11, 14)
        for d in DIMS:
            three[d].wait_recv()
        half[XYZ] = core_fwd(XYZ)
        work(14, 15)
        half[XYZ].wait_recv()
        work(15, 16)

    wh = wh_ref[...].astype(BF16)

    def layer_one(lo, hi):
        for s in range(lo, hi):
            a_copies[s].wait()

        def body(s, carry):
            hid[...] = jnp.dot(xg[s], wh, preferred_element_type=F32).astype(BF16)
            z1[...] += jnp.dot(a_v[s], hid[...], preferred_element_type=F32)
            return carry

        lax.fori_loop(lo, hi, body, 0)

    gather(AG_X, xg, ((0, 352), (352, 336), (688, 336)), layer_one)

    hid[...] = jnp.maximum(z1[...], 0.0).astype(BF16)
    tm = tm_ref[...].astype(F32)
    y2t = jnp.transpose(jnp.dot(hid[...], wop[...], preferred_element_type=F32))[:CP]
    row = lax.broadcasted_iota(jnp.int32, (CP, BR), 0)
    yg[0] = jnp.where(row == NC, tm, y2t).astype(BF16)

    first = [True]

    def layer_two(lo, hi):
        def body(s, carry):
            z2[:, :CP] += lax.dot_general(a_v[s], yg[s], LAST, preferred_element_type=F32)
            return carry

        lax.fori_loop(lo, hi, body, 0)
        if first[0]:
            first[0] = False
            pos[...] = jnp.where(jnp.transpose(z1[...]) > 0, 1.0, 0.0).astype(BF16)

    gather(AG_Y, yg, ((0, 16), (16, 16), (32, 16)), layer_two)

    count = jnp.zeros((1, BR), F32)
    for s in range(NB):
        count = count + yg[s, NC:CP, :].astype(F32)
    total = jnp.sum(count, axis=1, keepdims=True)
    zt = jnp.transpose(z2[...])[:CP]
    valid = row < NC
    top = jnp.max(jnp.where(valid, zt, -jnp.inf), axis=0, keepdims=True)
    lse = top + jnp.log(jnp.sum(jnp.where(valid, jnp.exp(zt - top), 0.0), axis=0, keepdims=True))
    hot = row == lab_ref[...]
    picked = jnp.sum(jnp.where(hot, zt, 0.0), axis=0, keepdims=True)
    loss = jnp.sum(tm * (lse - picked), axis=1, keepdims=True)
    grad = (jnp.exp(zt - lse) - hot.astype(F32)) * (tm / total)
    gt = jnp.where(valid, grad, 0.0).astype(BF16)

    def scatter(base, r, ra, rb, rc, pieces, left, stages, early):
        def rows(i):
            return pl.ds(*pieces[i])

        pair = {}

        def produce(k, q):
            st = stages(k)
            if not early and k >= 2:
                pair[k - 2].wait_send()
                sent[:] = [cp for cp in sent if cp is not pair[k - 2]]
            st[...] = jnp.dot(left, a_v[SLOT[q, 1]], preferred_element_type=F32)
            pair[k] = start(rcopy(st, r.at[q], base + k, 1))
            own = jnp.dot(left, a_v[SLOT[q, 0]], preferred_element_type=F32)
            pair[k].wait_recv()
            r[q] = r[q] + own

        def send(q, i, dst, k, d):
            return start(rcopy(r.at[q, rows(i)], dst, k, 2 * d))

        three, two, one = {}, {}, {}
        produce(0, XYZ)
        for i, d in enumerate(DIMS):
            three[d] = send(XYZ, i, ra.at[rows(i)], base + 8 + i, d)
        for k, d in enumerate(DIMS):
            q = d + NEXT[d]
            produce(1 + k, q)
            for i, e in enumerate(DIMS):
                if e + q != XYZ:
                    two[d, i] = send(q, i, rb.at[k, rows(i)], base + 11 + 3 * k + i, d)

        def outer():
            for i, e in enumerate(DIMS):
                three[e].wait_recv()
                q = XYZ - e
                r[q, rows(i)] = r[q, rows(i)] + ra[rows(i)]
                d = NEXT[e]
                k = DIMS.index(d)
                two[d, i] = send(q, i, rb.at[k, rows(i)], base + 11 + 3 * k + i, d)

        def inner():
            for j in range(3):
                for n, e in enumerate(DIMS):
                    d = PREV[e]
                    k = DIMS.index(d)
                    last = DIMS.index(XYZ - d - NEXT[d])
                    i = (last + 1 + j) % 3
                    two[d, i].wait_recv()
                    r[e, rows(i)] = r[e, rows(i)] + rb[k, rows(i)]
                    one[e, i] = send(e, i, rc.at[n, rows(i)], base + 20 + 3 * n + i, e)

        if early:
            outer()
        for k, d in enumerate(DIMS):
            produce(4 + k, d)
        if early:
            inner()
            produce(7, 0)
        else:
            produce(7, 0)
            outer()
            inner()
        for j in range(3):
            for n, e in enumerate(DIMS):
                i = (DIMS.index(XYZ - PREV[e] - e) + 1 + j) % 3
                one[e, i].wait_recv()
                r[0, rows(i)] = r[0, rows(i)] + rc[n, rows(i)]

    def stage_d2(k):
        return stage.at[k // 4, pl.ds(CP * (k % 4), CP)]

    scatter(RS_D2, r2, ra2, rb2, rc2, ((0, 16), (16, 16), (32, 16)), gt, stage_d2, True)

    d2t = r2[0].astype(BF16)
    for cp in sent:
        cp.wait_send()
    sent.clear()
    grad_hid = jnp.dot(wop[:, :CP], d2t, preferred_element_type=F32)
    pos[...] = jnp.where(pos[...] > 0, grad_hid, 0.0).astype(BF16)
    gwo_t = jnp.dot(d2t, hid[...], preferred_element_type=F32)
    gwo = jnp.transpose(jnp.concatenate([gwo_t, jnp.zeros((128 - CP, HID), F32)], axis=0))
    lane = lax.broadcasted_iota(jnp.int32, (HID, 128), 1)
    gwo = jnp.where(lane == LOSS_LANE, loss, gwo)
    for i in range(NB):
        fsrc[i, 16:32, :] = gwo[16 * i:16 * i + 16]

    def stage_d1(k):
        return stage.at[k % 2]

    scatter(RS_D1, r1, ra1, rb1, rc1, ((0, 88), (88, 88), (176, 80)), pos[...], stage_d1, False)

    d1t = r1[0].astype(BF16)
    gwh_t = jnp.dot(d1t, xg[0], preferred_element_type=F32)
    for i in range(NB):
        fsrc[i, 0:16, 0:FI] = gwh_t[16 * i:16 * i + 16]
    out_copies = [start(rcopy(fsrc.at[devs[m]], frecv.at[m], AR + m - 1, m)) for m in range(1, 16)]
    acc = fsrc[me]
    for m in range(1, 16):
        out_copies[m - 1].wait_recv()
        acc = acc + frecv[m]
    fsum[...] = acc
    fall[me] = acc
    for m in range(1, 16):
        start(rcopy(fsum, fall.at[me], AR + 15 + m - 1, m))
    for m in range(1, 16):
        rcopy(fsum, fall.at[devs[m]], AR + 15 + m - 1, m).wait_recv()
    gwh_all = jnp.concatenate([fall[i, 0:16, :] for i in range(NB)], axis=0)
    gwh_ref[...] = jnp.transpose(gwh_all)[:FI]
    for i in range(NB):
        gwo_ref[16 * i:16 * i + 16, :] = fall[i, 16:32, 0:NC]
    loss_ref[...] = fall[0, 16:17, LOSS_LANE:LOSS_LANE + 1] / total
    for cp in sent:
        cp.wait_send()


def device_step(adj_rows, feat_rows, w_hidden, w_output, labels, train_mask, block_mask):
    del block_mask
    vmem = pl.BlockSpec(memory_space=pltpu.VMEM)
    hbm = pl.BlockSpec(memory_space=pl.ANY)
    loss, gwh, gwo = pl.pallas_call(
        kernel,
        out_shape=(
            jax.ShapeDtypeStruct((1, 1), F32),
            jax.ShapeDtypeStruct((FI, HID), F32),
            jax.ShapeDtypeStruct((HID, NC), F32),
        ),
        in_specs=[hbm, hbm, vmem, vmem, vmem, vmem],
        out_specs=(vmem, vmem, vmem),
        scratch_shapes=[
            pltpu.VMEM((NB, BR, BR), BF16),
            pltpu.VMEM((NB, BR, FI), BF16),
            pltpu.VMEM((NB, CP, BR), BF16),
            pltpu.VMEM((BR, HID), F32),
            pltpu.VMEM((BR, HID), BF16),
            pltpu.VMEM((HID, BR), BF16),
            pltpu.VMEM((BR, 128), F32),
            pltpu.VMEM((8, CP, BR), F32),
            pltpu.VMEM((CP, BR), F32),
            pltpu.VMEM((3, CP, BR), F32),
            pltpu.VMEM((3, CP, BR), F32),
            pltpu.VMEM((8, HID, BR), F32),
            pltpu.VMEM((HID, BR), F32),
            pltpu.VMEM((3, HID, BR), F32),
            pltpu.VMEM((3, HID, BR), F32),
            pltpu.VMEM((2, HID, BR), F32),
            pltpu.VMEM((HID, 128), BF16),
            pltpu.VMEM((NB, 32, 128), F32),
            pltpu.VMEM((NB, 32, 128), F32),
            pltpu.VMEM((32, 128), F32),
            pltpu.VMEM((NB, 32, 128), F32),
            pltpu.SemaphoreType.DMA((NB,)),
            pltpu.SemaphoreType.DMA,
            pltpu.SemaphoreType.DMA((N_SEM,)),
            pltpu.SemaphoreType.DMA((N_SEM,)),
        ],
        compiler_params=pltpu.CompilerParams(
            collective_id=0, has_side_effects=True, vmem_limit_bytes=67_043_328),
        name='gcn_step',
    )(adj_rows, feat_rows, w_hidden, w_output, labels.reshape(1, -1), train_mask.reshape(1, -1))
    return loss[0, 0], gwh, gwo


def solution(mesh):
    row_spec = P(AXIS, None)
    vec_spec = P(AXIS)
    return jax.shard_map(
        device_step, mesh=mesh,
        in_specs=(row_spec, row_spec, P(), P(), vec_spec, vec_spec, P()),
        out_specs=(P(), P(), P()), check_vma=False)
```

time: 513 us -> 153 us (0.30)
  waiting for transfers between devices: 343 us -> 0 us
  Pallas kernels: 0 us -> 144 us
  matrix products: 71.2 us -> 0 us
  blocking collectives: 63.7 us -> 0 us
  between operations: 16.4 us -> 2.39 us
  other arithmetic: 10.8 us -> 0 us
    reduce_scatter x2 -> x0, waiting for transfers between devices: 231 us -> none  [transpose_product_scatter(): lax.psum_scatter(contrib.reshape(-1, width), AXIS_NAME, scatter_dimension...]
    pallas_call x0 -> x1, Pallas kernels: none -> 144 us  [device_step(): pl.pallas_call(kernel, out_shape=(jax.ShapeDtypeStruct((1, 1), F32), jax....]
    all_gather x2 -> x0, waiting for transfers between devices: 78.2 us -> none  [gather_masked(): gathered = lax.all_gather(local_vals, AXIS_NAME, axis=0, tiled=False)]
    dot_general x8 -> x0, matrix products: 71.2 us -> none  [the longest x2 34 us: transpose_product_scatter(): lax.dot_general(adj_rows, local_grad, ROW_CONTRACT, preferred_element_typ...]
    psum x2 -> x0, blocking collectives: 63.7 us -> none  [the longest x1 31.9 us: device_step(): lax.psum(lax.dot_general(hidden, grad_proj_two, ROW_CONTRACT, preferred_e...]
    psum x1 -> x0, waiting for transfers between devices: 33.5 us -> none  [device_step(): lax.psum(lax.dot_general(feat_rows, grad_proj_one, ROW_CONTRACT, preferre...]
    mul x1 -> x0, other arithmetic: 7.2 us -> none  [gather_masked(): gathered = gathered * mask_row.astype(local_vals.dtype)[:, None, None]]
  transfers between devices with their start and end apart: 5 -> 0, of which waited for: 5 -> 0; matrix products, arithmetic and copies ran while one was open for 0% -> 0% of each run, Pallas kernels for 0% -> 0%
where the time goes in v1:
time: 153 us; the launch traced here: 152 us
  Pallas kernels  144 us (94%)
  local copies, waits for them, and re-layouts  6.5 us (4%)
  between operations  2.39 us (2%)
    pallas_call x1, Pallas kernels, device_step(): pl.pallas_call(kernel, out_shape=(jax.ShapeDtypeStruct((1, 1), F32), jax....  144 us
    unnamed x4, local copies, waits for them, and re-layouts  6.5 us

profile of v1, /device:TPU:0, one launch (start us, length us, event | category | flops | bytes accessed | tf_op | source)
XLA Modules:
  0.0 152.4 jit_solution(17764594064246806076)
XLA Ops:
  0.6 1.6 %copy.10.wo_ref = f32[256,47]{1,0:T(8,128)} copy(f32[256,47]{0,1:T(8,128)} %param.10) | data formatting | bytes 96256 | tf_op args[3]
  2.2 1.8 %copy.9.x_hbm = bf16[1024,100]{1,0:T(8,128)(2,1)} copy(bf16[1024,100]{0,1:T(8,128)(2,1)} %param.8) | data formatting | bytes 409600 | tf_op args[1]
  4.0 143.6 %gcn_step.1 = (f32[1,1]{1,0:T(1,128)}, f32[100,256]{1,0:T(8,128)}, f32[256,47]{1,0:T(8,128)}) custom-call(bf16[1024,16384]{1,0:T(8,128)(2,1)} %a_hbm.1, bf16[1024,100]{1,0:T(8,128)(2,1)} %copy.9.x_hbm, f32[100,256]{1,0:T(8,128)} %wh_ref.1, f32[256,47]{1,0:T(8,128)} %copy.10.wo_ref, s32[1,1024]{1,0:T(1,128)} %bitcast.3, s32[1,1024]{1,0:T(1,128)} %bitcast.4), custom_call_target="tpu_custom_call" | custom-call | tf_op jit(solution)/shard_map/gcn_step/pallas_call | solution.py:288
  147.5 1.6 %copy.11 = f32[256,47]{0,1:T(8,128)} copy(f32[256,47]{1,0:T(8,128)} %get-tuple-element.11) | data formatting | bytes 96256
  149.8 1.5 %copy.15 = f32[100,256]{1,0:T(8,128)} copy(f32[100,256]{1,0:T(8,128)} %get-tuple-element.16) | data formatting | bytes 204800

commit v2 on v1

--- a/solution.py
+++ b/solution.py
@@ -10,6 +10,7 @@
 AXIS = 'nodes'
 MESH = pl.DeviceIdType.MESH
 F32, BF16 = jnp.float32, jnp.bfloat16
+FIRST = (((0,), (0,)), ((), ()))
 LAST = (((1,), (1,)), ((), ()))
 NB, BR, FI, HID, NC, CP = 16, 1024, 100, 256, 47, 48
 X, Y, Z = 1, 2, 4
@@ -40,8 +41,8 @@
 
 
 def kernel(a_hbm, x_hbm, wh_ref, wo_ref, lab_ref, tm_ref,
-           loss_ref, gwh_ref, gwo_ref,
-           a_v, xg, yg, z1, hid, pos, z2, r2, ra2, rb2, rc2, r1, ra1, rb1, rc1, stage, wop,
+           sums_ref, count_ref,
+           a_v, xg, yg, y1, z1, hid, pos, z2, r2, ra2, rb2, rc2, r1, ra1, rb1, rc1, stage, wop,
            fsrc, frecv, fsum, fall, a_sem, x_sem, send_sem, recv_sem):
     me = lax.axis_index(AXIS)
     devs = {m: peer(me, m) for m in range(16)}
@@ -61,14 +62,14 @@
         cp.start()
 
     barrier = pltpu.get_barrier_semaphore()
-    for m in range(1, 16):
+    for m in (1, 2, 4, 8):
         pl.semaphore_signal(barrier, inc=1, device_id=(devs[m],), device_id_type=MESH)
     wop[...] = jnp.zeros_like(wop)
-    wop[:, :NC] = wo_ref[...].astype(BF16)
+    wop[:NC] = wo_ref[...].astype(BF16)
     fsrc[...] = jnp.zeros_like(fsrc)
     z2[...] = jnp.zeros_like(z2)
     z1[...] = jnp.zeros_like(z1)
-    pl.semaphore_wait(barrier, 15)
+    pl.semaphore_wait(barrier, 4)
     x_copy.wait()
 
     sent = []
@@ -78,23 +79,26 @@
         sent.append(cp)
         return cp
 
-    def gather(base, g, pieces, work):
+    def gather(base, g, pieces, work, early):
         def core_fwd(q):
             return start(rcopy(g.at[SLOT[q, 0]], g.at[SLOT[q, 1]], base + 9 + q, 1))
 
         one = {d: start(rcopy(g.at[0], g.at[SLOT[d, 0]], base + i, 2 * d)) for i, d in enumerate(DIMS)}
         half = {0: core_fwd(0)}
-        work(0, 1)
-        half[0].wait_recv()
-        work(1, 2)
         two, three = {}, {}
-        for d in DIMS:
-            one[d].wait_recv()
+        for n in range(early):
+            work(n, n + 1)
+            if n == 0:
+                half[0].wait_recv()
         for i, d in enumerate(DIMS):
             e = NEXT[d]
+            one[e].wait_recv()
             two[d] = start(rcopy(g.at[SLOT[e, 0]], g.at[SLOT[d + e, 0]], base + 3 + i, 2 * d))
         for d in DIMS:
             half[d] = core_fwd(d)
+        if not early:
+            half[0].wait_recv()
+            work(0, 2)
         work(2, 5)
         for d in DIMS:
             half[d].wait_recv()
@@ -123,18 +127,20 @@
         for s in range(lo, hi):
             a_copies[s].wait()
 
-        def body(s, carry):
-            hid[...] = jnp.dot(xg[s], wh, preferred_element_type=F32).astype(BF16)
-            z1[...] += jnp.dot(a_v[s], hid[...], preferred_element_type=F32)
-            return carry
-
-        lax.fori_loop(lo, hi, body, 0)
-
-    gather(AG_X, xg, ((0, 352), (352, 336), (688, 336)), layer_one)
+        def proj(s, ref):
+            ref[...] = lax.dot_general(xg[s], wh, FIRST, preferred_element_type=F32).astype(BF16)
+
+        bufs = (hid, y1.at[0], y1.at[1])
+        for n, s in enumerate(range(lo, hi)):
+            proj(s, bufs[n])
+        for n, s in enumerate(range(lo, hi)):
+            z1[...] += jnp.dot(a_v[s], bufs[n][...], preferred_element_type=F32)
+
+    gather(AG_X, xg, ((0, 32), (32, 32), (64, 36)), layer_one, 0)
 
     hid[...] = jnp.maximum(z1[...], 0.0).astype(BF16)
     tm = tm_ref[...].astype(F32)
-    y2t = jnp.transpose(jnp.dot(hid[...], wop[...], preferred_element_type=F32))[:CP]
+    y2t = lax.dot_general(wop[...], hid[...], LAST, preferred_element_type=F32)
     row = lax.broadcasted_iota(jnp.int32, (CP, BR), 0)
     yg[0] = jnp.where(row == NC, tm, y2t).astype(BF16)
 
@@ -150,7 +156,7 @@
             first[0] = False
             pos[...] = jnp.where(jnp.transpose(z1[...]) > 0, 1.0, 0.0).astype(BF16)
 
-    gather(AG_Y, yg, ((0, 16), (16, 16), (32, 16)), layer_two)
+    gather(AG_Y, yg, ((0, 16), (16, 16), (32, 16)), layer_two, 2)
 
     count = jnp.zeros((1, BR), F32)
     for s in range(NB):
@@ -172,27 +178,36 @@
 
         pair = {}
 
-        def produce(k, q):
+        def other(k, q):
             st = stages(k)
             if not early and k >= 2:
                 pair[k - 2].wait_send()
                 sent[:] = [cp for cp in sent if cp is not pair[k - 2]]
             st[...] = jnp.dot(left, a_v[SLOT[q, 1]], preferred_element_type=F32)
             pair[k] = start(rcopy(st, r.at[q], base + k, 1))
-            own = jnp.dot(left, a_v[SLOT[q, 0]], preferred_element_type=F32)
+
+        def own(k, q):
             pair[k].wait_recv()
-            r[q] = r[q] + own
+            r[q] = r[q] + jnp.dot(left, a_v[SLOT[q, 0]], preferred_element_type=F32)
 
         def send(q, i, dst, k, d):
             return start(rcopy(r.at[q, rows(i)], dst, k, 2 * d))
 
         three, two, one = {}, {}, {}
-        produce(0, XYZ)
+        order = (XYZ,) + tuple(d + NEXT[d] for d in DIMS) + DIMS + (0,)
+
+        def produce(k):
+            if k < 7:
+                other(k + 1, order[k + 1])
+            own(k, order[k])
+
+        other(0, XYZ)
+        produce(0)
         for i, d in enumerate(DIMS):
             three[d] = send(XYZ, i, ra.at[rows(i)], base + 8 + i, d)
         for k, d in enumerate(DIMS):
             q = d + NEXT[d]
-            produce(1 + k, q)
+            produce(1 + k)
             for i, e in enumerate(DIMS):
                 if e + q != XYZ:
                     two[d, i] = send(q, i, rb.at[k, rows(i)], base + 11 + 3 * k + i, d)
@@ -220,12 +235,12 @@
         if early:
             outer()
         for k, d in enumerate(DIMS):
-            produce(4 + k, d)
+            produce(4 + k)
         if early:
             inner()
-            produce(7, 0)
+            produce(7)
         else:
-            produce(7, 0)
+            produce(7)
             outer()
             inner()
         for j in range(3):
@@ -243,7 +258,7 @@
     for cp in sent:
         cp.wait_send()
     sent.clear()
-    grad_hid = jnp.dot(wop[:, :CP], d2t, preferred_element_type=F32)
+    grad_hid = lax.dot_general(wop[...], d2t, FIRST, preferred_element_type=F32)
     pos[...] = jnp.where(pos[...] > 0, grad_hid, 0.0).astype(BF16)
     gwo_t = jnp.dot(d2t, hid[...], preferred_element_type=F32)
     gwo = jnp.transpose(jnp.concatenate([gwo_t, jnp.zeros((128 - CP, HID), F32)], axis=0))
@@ -258,7 +273,7 @@
     scatter(RS_D1, r1, ra1, rb1, rc1, ((0, 88), (88, 88), (176, 80)), pos[...], stage_d1, False)
 
     d1t = r1[0].astype(BF16)
-    gwh_t = jnp.dot(d1t, xg[0], preferred_element_type=F32)
+    gwh_t = lax.dot_general(d1t, xg[0], LAST, preferred_element_type=F32)
     for i in range(NB):
         fsrc[i, 0:16, 0:FI] = gwh_t[16 * i:16 * i + 16]
     out_copies = [start(rcopy(fsrc.at[devs[m]], frecv.at[m], AR + m - 1, m)) for m in range(1, 16)]
@@ -272,32 +287,38 @@
         start(rcopy(fsum, fall.at[me], AR + 15 + m - 1, m))
     for m in range(1, 16):
         rcopy(fsum, fall.at[devs[m]], AR + 15 + m - 1, m).wait_recv()
-    gwh_all = jnp.concatenate([fall[i, 0:16, :] for i in range(NB)], axis=0)
-    gwh_ref[...] = jnp.transpose(gwh_all)[:FI]
     for i in range(NB):
-        gwo_ref[16 * i:16 * i + 16, :] = fall[i, 16:32, 0:NC]
-    loss_ref[...] = fall[0, 16:17, LOSS_LANE:LOSS_LANE + 1] / total
+        sums_ref[i] = fall[i]
+    count_ref[...] = total
     for cp in sent:
         cp.wait_send()
+
+
+def unpack(sums_ref, count_ref, loss_ref, gwh_ref, gwo_ref):
+    gwh = jnp.concatenate([sums_ref[i, 0:16, :] for i in range(NB)], axis=0)
+    gwo = jnp.concatenate([sums_ref[i, 16:32, :] for i in range(NB)], axis=0)
+    gwh_ref[...] = jnp.transpose(gwh)[:FI]
+    gwo_ref[...] = jnp.transpose(gwo)[:NC]
+    loss_ref[...] = gwo[0:1, LOSS_LANE:LOSS_LANE + 1] / count_ref[...]
 
 
 def device_step(adj_rows, feat_rows, w_hidden, w_output, labels, train_mask, block_mask):
     del block_mask
     vmem = pl.BlockSpec(memory_space=pltpu.VMEM)
     hbm = pl.BlockSpec(memory_space=pl.ANY)
-    loss, gwh, gwo = pl.pallas_call(
+    sums, count = pl.pallas_call(
         kernel,
         out_shape=(
+            jax.ShapeDtypeStruct((NB, 32, 128), F32),
             jax.ShapeDtypeStruct((1, 1), F32),
-            jax.ShapeDtypeStruct((FI, HID), F32),
-            jax.ShapeDtypeStruct((HID, NC), F32),
         ),
         in_specs=[hbm, hbm, vmem, vmem, vmem, vmem],
-        out_specs=(vmem, vmem, vmem),
+        out_specs=(vmem, vmem),
         scratch_shapes=[
             pltpu.VMEM((NB, BR, BR), BF16),
-            pltpu.VMEM((NB, BR, FI), BF16),
+            pltpu.VMEM((NB, FI, BR), BF16),
             pltpu.VMEM((NB, CP, BR), BF16),
+            pltpu.VMEM((2, BR, HID), BF16),
             pltpu.VMEM((BR, HID), F32),
             pltpu.VMEM((BR, HID), BF16),
             pltpu.VMEM((HID, BR), BF16),
@@ -311,7 +332,7 @@
             pltpu.VMEM((3, HID, BR), F32),
             pltpu.VMEM((3, HID, BR), F32),
             pltpu.VMEM((2, HID, BR), F32),
-            pltpu.VMEM((HID, 128), BF16),
+            pltpu.VMEM((CP, HID), BF16),
             pltpu.VMEM((NB, 32, 128), F32),
             pltpu.VMEM((NB, 32, 128), F32),
             pltpu.VMEM((32, 128), F32),
@@ -324,8 +345,19 @@
         compiler_params=pltpu.CompilerParams(
             collective_id=0, has_side_effects=True, vmem_limit_bytes=67_043_328),
         name='gcn_step',
-    )(adj_rows, feat_rows, w_hidden, w_output, labels.reshape(1, -1), train_mask.reshape(1, -1))
-    return loss[0, 0], gwh, gwo
+    )(adj_rows, feat_rows.T, w_hidden, w_output.T, labels.reshape(1, -1), train_mask.reshape(1, -1))
+    loss, gwh, gwo = pl.pallas_call(
+        unpack,
+        out_shape=(
+            jax.ShapeDtypeStruct((1, 1), F32),
+            jax.ShapeDtypeStruct((FI, HID), F32),
+            jax.ShapeDtypeStruct((NC, HID), F32),
+        ),
+        in_specs=[vmem, vmem],
+        out_specs=(vmem, vmem, vmem),
+        name='unpack',
+    )(sums, count)
+    return loss[0, 0], gwh, gwo.T
 
 
 def solution(mesh):

time: 153 us -> 148 us (0.967)
  local copies, waits for them, and re-layouts: 6.5 us -> 0 us
  Pallas kernels: 144 us -> 147 us
  between operations: 2.39 us -> 0.64 us
    unnamed x4 -> x0, local copies, waits for them, and re-layouts: 6.5 us -> none
    pallas_call x1 -> x2, Pallas kernels: 144 us -> 147 us  [the longest x1 145 us: device_step(): pl.pallas_call(kernel, out_shape=(jax.ShapeDtypeStruct((NB, 32, 128), F32...]
where the time goes in v2:
time: 148 us
  Pallas kernels  147 us (99%)
    pallas_call x1, Pallas kernels, device_step(): pl.pallas_call(kernel, out_shape=(jax.ShapeDtypeStruct((NB, 32, 128), F32...  145 us

profile of v2, /device:TPU:0, one launch (start us, length us, event | category | flops | bytes accessed | tf_op | source)
XLA Modules:
  0.0 147.7 jit_solution(959091603750161165)
XLA Ops:
  0.6 144.8 %gcn_step.1 = (f32[16,32,128]{2,1,0:T(8,128)}, f32[1,1]{1,0:T(1,128)}) custom-call(bf16[1024,16384]{1,0:T(8,128)(2,1)} %a_hbm.1, bf16[100,1024]{1,0:T(8,128)(2,1)} %bitcast.6, f32[100,256]{1,0:T(8,128)} %wh_ref.1, f32[47,256]{1,0:T(8,128)} %bitcast.7, s32[1,1024]{1,0:T(1,128)} %bitcast.8, s32[1,1024]{1,0:T(1,128)} %bitcast.9), custom_call_target="tpu_custom_call" | custom-call | tf_op jit(solution)/shard_map/gcn_step/pallas_call | solution.py:309
  145.4 2.3 %unpack.1 = (f32[1,1]{1,0:T(1,128)}, f32[100,256]{1,0:T(8,128)}, f32[47,256]{1,0:T(8,128)}) custom-call(f32[16,32,128]{2,1,0:T(8,128)} %get-tuple-element.8.sums_ref, f32[1,1]{1,0:T(1,128)} %get-tuple-element.9.count_ref), custom_call_target="tpu_custom_call" | custom-call | tf_op jit(solution)/shard_map/unpack/pallas_call | solution.py:349

commit v3 on v2

--- a/solution.py
+++ b/solution.py
@@ -29,7 +29,7 @@
 AG_X, AG_Y = 0, AG_COPIES
 RS_D2, RS_D1 = 2 * AG_COPIES, 2 * AG_COPIES + RS_COPIES
 AR = 2 * AG_COPIES + 2 * RS_COPIES
-N_SEM = AR + 30
+N_SEM = AR + 60
 
 
 def peer(me, mask):
@@ -58,17 +58,13 @@
         a_copies.append(pltpu.make_async_copy(a_hbm.at[:, pl.ds(col, BR)], a_v.at[s], a_sem.at[s]))
     x_copy = pltpu.make_async_copy(x_hbm, xg.at[0], x_sem)
     x_copy.start()
-    for cp in a_copies:
-        cp.start()
 
     barrier = pltpu.get_barrier_semaphore()
     for m in (1, 2, 4, 8):
         pl.semaphore_signal(barrier, inc=1, device_id=(devs[m],), device_id_type=MESH)
     wop[...] = jnp.zeros_like(wop)
     wop[:NC] = wo_ref[...].astype(BF16)
-    fsrc[...] = jnp.zeros_like(fsrc)
     z2[...] = jnp.zeros_like(z2)
-    z1[...] = jnp.zeros_like(z1)
     pl.semaphore_wait(barrier, 4)
     x_copy.wait()
 
@@ -79,49 +75,51 @@
         sent.append(cp)
         return cp
 
-    def gather(base, g, pieces, work, early):
+    def gather(base, g, pieces, work, load):
         def core_fwd(q):
             return start(rcopy(g.at[SLOT[q, 0]], g.at[SLOT[q, 1]], base + 9 + q, 1))
 
         one = {d: start(rcopy(g.at[0], g.at[SLOT[d, 0]], base + i, 2 * d)) for i, d in enumerate(DIMS)}
         half = {0: core_fwd(0)}
         two, three = {}, {}
-        for n in range(early):
-            work(n, n + 1)
-            if n == 0:
-                half[0].wait_recv()
+        load(0)
+        work(0, 1)
+        half[0].wait_recv()
+        work(1, 2)
         for i, d in enumerate(DIMS):
             e = NEXT[d]
             one[e].wait_recv()
             two[d] = start(rcopy(g.at[SLOT[e, 0]], g.at[SLOT[d + e, 0]], base + 3 + i, 2 * d))
         for d in DIMS:
             half[d] = core_fwd(d)
-        if not early:
-            half[0].wait_recv()
-            work(0, 2)
+        load(1)
         work(2, 5)
         for d in DIMS:
             half[d].wait_recv()
         work(5, 8)
-        for d in DIMS:
-            two[d].wait_recv()
         for i, d in enumerate(DIMS):
             rows = pl.ds(*pieces[i])
+            two[NEXT[d]].wait_recv()
             three[d] = start(rcopy(g.at[SLOT[XYZ - d, 0], rows], g.at[SLOT[XYZ, 0], rows], base + 6 + i, 2 * d))
         for d in DIMS:
             half[XYZ - d] = core_fwd(XYZ - d)
         work(8, 11)
         for d in DIMS:
+            three[d].wait_recv()
+        half[XYZ] = core_fwd(XYZ)
+        for d in DIMS:
             half[XYZ - d].wait_recv()
         work(11, 14)
-        for d in DIMS:
-            three[d].wait_recv()
-        half[XYZ] = core_fwd(XYZ)
-        work(14, 15)
         half[XYZ].wait_recv()
-        work(15, 16)
+        work(14, 16)
 
     wh = wh_ref[...].astype(BF16)
+
+    def load_a(part):
+        for s in range(8 * part, 8 * part + 8):
+            a_copies[s].start()
+        if part == 0:
+            z1[...] = jnp.zeros_like(z1)
 
     def layer_one(lo, hi):
         for s in range(lo, hi):
@@ -136,7 +134,7 @@
         for n, s in enumerate(range(lo, hi)):
             z1[...] += jnp.dot(a_v[s], bufs[n][...], preferred_element_type=F32)
 
-    gather(AG_X, xg, ((0, 32), (32, 32), (64, 36)), layer_one, 0)
+    gather(AG_X, xg, ((0, 32), (32, 32), (64, 36)), layer_one, load_a)
 
     hid[...] = jnp.maximum(z1[...], 0.0).astype(BF16)
     tm = tm_ref[...].astype(F32)
@@ -151,12 +149,16 @@
             z2[:, :CP] += lax.dot_general(a_v[s], yg[s], LAST, preferred_element_type=F32)
             return carry
 
-        lax.fori_loop(lo, hi, body, 0)
+        if 2 <= lo < 8:
+            lax.fori_loop(lo, hi, body, 0)
+        else:
+            for s in range(lo, hi):
+                body(s, 0)
         if first[0]:
             first[0] = False
             pos[...] = jnp.where(jnp.transpose(z1[...]) > 0, 1.0, 0.0).astype(BF16)
 
-    gather(AG_Y, yg, ((0, 16), (16, 16), (32, 16)), layer_two, 2)
+    gather(AG_Y, yg, ((0, 16), (16, 16), (32, 16)), layer_two, lambda part: None)
 
     count = jnp.zeros((1, BR), F32)
     for s in range(NB):
@@ -172,7 +174,7 @@
     grad = (jnp.exp(zt - lse) - hot.astype(F32)) * (tm / total)
     gt = jnp.where(valid, grad, 0.0).astype(BF16)
 
-    def scatter(base, r, ra, rb, rc, pieces, left, stages, early):
+    def scatter(base, r, ra, rb, rc, pieces, left, stages, early, middle, late):
         def rows(i):
             return pl.ds(*pieces[i])
 
@@ -183,12 +185,31 @@
             if not early and k >= 2:
                 pair[k - 2].wait_send()
                 sent[:] = [cp for cp in sent if cp is not pair[k - 2]]
-            st[...] = jnp.dot(left, a_v[SLOT[q, 1]], preferred_element_type=F32)
+            if early or k == 0:
+                st[...] = jnp.dot(left[...], a_v[SLOT[q, 1]], preferred_element_type=F32)
+            else:
+                def body(h, carry):
+                    cols = pl.ds(pl.multiple_of(h * 512, 512), 512)
+                    st[:, cols] = jnp.dot(left[...], a_v[SLOT[q, 1], :, cols], preferred_element_type=F32)
+                    return carry
+
+                lax.fori_loop(0, 2, body, 0)
             pair[k] = start(rcopy(st, r.at[q], base + k, 1))
 
         def own(k, q):
-            pair[k].wait_recv()
-            r[q] = r[q] + jnp.dot(left, a_v[SLOT[q, 0]], preferred_element_type=F32)
+            if early:
+                mine = jnp.dot(left[...], a_v[SLOT[q, 0]], preferred_element_type=F32)
+                pair[k].wait_recv()
+                r[q] = r[q] + mine
+            else:
+                pair[k].wait_recv()
+
+                def body(h, carry):
+                    cols = pl.ds(pl.multiple_of(h * 512, 512), 512)
+                    r[q, :, cols] = r[q, :, cols] + jnp.dot(left[...], a_v[SLOT[q, 0], :, cols], preferred_element_type=F32)
+                    return carry
+
+                lax.fori_loop(0, 2, body, 0)
 
         def send(q, i, dst, k, d):
             return start(rcopy(r.at[q, rows(i)], dst, k, 2 * d))
@@ -241,8 +262,10 @@
             produce(7)
         else:
             produce(7)
+            middle()
             outer()
             inner()
+        late()
         for j in range(3):
             for n, e in enumerate(DIMS):
                 i = (DIMS.index(XYZ - PREV[e] - e) + 1 + j) % 3
@@ -252,7 +275,7 @@
     def stage_d2(k):
         return stage.at[k // 4, pl.ds(CP * (k % 4), CP)]
 
-    scatter(RS_D2, r2, ra2, rb2, rc2, ((0, 16), (16, 16), (32, 16)), gt, stage_d2, True)
+    scatter(RS_D2, r2, ra2, rb2, rc2, ((0, 16), (16, 16), (32, 16)), gt, stage_d2, True, None, lambda: None)
 
     d2t = r2[0].astype(BF16)
     for cp in sent:
@@ -260,43 +283,56 @@
     sent.clear()
     grad_hid = lax.dot_general(wop[...], d2t, FIRST, preferred_element_type=F32)
     pos[...] = jnp.where(pos[...] > 0, grad_hid, 0.0).astype(BF16)
-    gwo_t = jnp.dot(d2t, hid[...], preferred_element_type=F32)
-    gwo = jnp.transpose(jnp.concatenate([gwo_t, jnp.zeros((128 - CP, HID), F32)], axis=0))
-    lane = lax.broadcasted_iota(jnp.int32, (HID, 128), 1)
-    gwo = jnp.where(lane == LOSS_LANE, loss, gwo)
-    for i in range(NB):
-        fsrc[i, 16:32, :] = gwo[16 * i:16 * i + 16]
+
+    parts = {}
+
+    def exchange(n, values):
+        for i in range(NB):
+            fsrc[n, i] = values[16 * i:16 * i + 16]
+        k = AR + 30 * n - 1
+        parts[n] = [start(rcopy(fsrc.at[n, devs[m]], frecv.at[n, m], k + m, m)) for m in range(1, 16)]
+
+    def share(n):
+        acc = fsrc[n, me]
+        for m in range(1, 16):
+            parts[n][m - 1].wait_recv()
+            acc = acc + frecv[n, m]
+        fsum[n] = acc
+        fall[n, me] = acc
+        for m in range(1, 16):
+            start(rcopy(fsum.at[n], fall.at[n, me], AR + 30 * n + 14 + m, m))
+
+    def collect(n):
+        for m in range(1, 16):
+            rcopy(fsum.at[n], fall.at[n, devs[m]], AR + 30 * n + 14 + m, m).wait_recv()
+
+    def middle():
+        gwo_t = jnp.dot(d2t, hid[...], preferred_element_type=F32)
+        gwo = jnp.transpose(jnp.concatenate([gwo_t, jnp.zeros((128 - CP, HID), F32)], axis=0))
+        lane = lax.broadcasted_iota(jnp.int32, (HID, 128), 1)
+        exchange(0, jnp.where(lane == LOSS_LANE, loss, gwo))
 
     def stage_d1(k):
         return stage.at[k % 2]
 
-    scatter(RS_D1, r1, ra1, rb1, rc1, ((0, 88), (88, 88), (176, 80)), pos[...], stage_d1, False)
+    scatter(RS_D1, r1, ra1, rb1, rc1, ((0, 88), (88, 88), (176, 80)), pos, stage_d1, False, middle, lambda: share(0))
 
     d1t = r1[0].astype(BF16)
     gwh_t = lax.dot_general(d1t, xg[0], LAST, preferred_element_type=F32)
-    for i in range(NB):
-        fsrc[i, 0:16, 0:FI] = gwh_t[16 * i:16 * i + 16]
-    out_copies = [start(rcopy(fsrc.at[devs[m]], frecv.at[m], AR + m - 1, m)) for m in range(1, 16)]
-    acc = fsrc[me]
-    for m in range(1, 16):
-        out_copies[m - 1].wait_recv()
-        acc = acc + frecv[m]
-    fsum[...] = acc
-    fall[me] = acc
-    for m in range(1, 16):
-        start(rcopy(fsum, fall.at[me], AR + 15 + m - 1, m))
-    for m in range(1, 16):
-        rcopy(fsum, fall.at[devs[m]], AR + 15 + m - 1, m).wait_recv()
-    for i in range(NB):
-        sums_ref[i] = fall[i]
+    exchange(1, jnp.concatenate([gwh_t, jnp.zeros((HID, 128 - FI), F32)], axis=1))
+    share(1)
+    collect(0)
+    collect(1)
+    for n in range(2):
+        for i in range(NB):
+            sums_ref[n, i] = fall[n, i]
     count_ref[...] = total
     for cp in sent:
         cp.wait_send()
 
 
 def unpack(sums_ref, count_ref, loss_ref, gwh_ref, gwo_ref):
-    gwh = jnp.concatenate([sums_ref[i, 0:16, :] for i in range(NB)], axis=0)
-    gwo = jnp.concatenate([sums_ref[i, 16:32, :] for i in range(NB)], axis=0)
+    gwo, gwh = (jnp.concatenate([sums_ref[n, i] for i in range(NB)], axis=0) for n in range(2))
     gwh_ref[...] = jnp.transpose(gwh)[:FI]
     gwo_ref[...] = jnp.transpose(gwo)[:NC]
     loss_ref[...] = gwo[0:1, LOSS_LANE:LOSS_LANE + 1] / count_ref[...]
@@ -309,7 +345,7 @@
     sums, count = pl.pallas_call(
         kernel,
         out_shape=(
-            jax.ShapeDtypeStruct((NB, 32, 128), F32),
+            jax.ShapeDtypeStruct((2, NB, 16, 128), F32),
             jax.ShapeDtypeStruct((1, 1), F32),
         ),
         in_specs=[hbm, hbm, vmem, vmem, vmem, vmem],
@@ -333,10 +369,10 @@
             pltpu.VMEM((3, HID, BR), F32),
             pltpu.VMEM((2, HID, BR), F32),
             pltpu.VMEM((CP, HID), BF16),
-            pltpu.VMEM((NB, 32, 128), F32),
-            pltpu.VMEM((NB, 32, 128), F32),
-            pltpu.VMEM((32, 128), F32),
-            pltpu.VMEM((NB, 32, 128), F32),
+            pltpu.VMEM((2, NB, 16, 128), F32),
+            pltpu.VMEM((2, NB, 16, 128), F32),
+            pltpu.VMEM((2, 16, 128), F32),
+            pltpu.VMEM((2, NB, 16, 128), F32),
             pltpu.SemaphoreType.DMA((NB,)),
             pltpu.SemaphoreType.DMA,
             pltpu.SemaphoreType.DMA((N_SEM,)),

time: 148 us -> 133 us (0.90)
  Pallas kernels: 147 us -> 133 us
    pallas_call x1, Pallas kernels: 145 us -> 130 us  [device_step(): pl.pallas_call(kernel, out_shape=(jax.ShapeDtypeStruct((2, NB, 16, 128),...]
where the time goes in v3:
time: 133 us
  Pallas kernels  133 us (100%)
    pallas_call x1, Pallas kernels, device_step(): pl.pallas_call(kernel, out_shape=(jax.ShapeDtypeStruct((2, NB, 16, 128),...  130 us

profile of v3, /device:TPU:0, one launch (start us, length us, event | category | flops | bytes accessed | tf_op | source)
XLA Modules:
  0.0 133.1 jit_solution(16170576525540265459)
XLA Ops:
  0.6 130.2 %gcn_step.1 = (f32[2,16,16,128]{3,2,1,0:T(8,128)}, f32[1,1]{1,0:T(1,128)}) custom-call(bf16[1024,16384]{1,0:T(8,128)(2,1)} %a_hbm.1, bf16[100,1024]{1,0:T(8,128)(2,1)} %bitcast.6, f32[100,256]{1,0:T(8,128)} %wh_ref.1, f32[47,256]{1,0:T(8,128)} %bitcast.7, s32[1,1024]{1,0:T(1,128)} %bitcast.8, s32[1,1024]{1,0:T(1,128)} %bitcast.9), custom_call_target="tpu_custom_call" | custom-call | tf_op jit(solution)/shard_map/gcn_step/pallas_call | solution.py:345
  130.9 2.3 %unpack.1 = (f32[1,1]{1,0:T(1,128)}, f32[100,256]{1,0:T(8,128)}, f32[47,256]{1,0:T(8,128)}) custom-call(f32[2,16,16,128]{3,2,1,0:T(8,128)} %get-tuple-element.8.sums_ref, f32[1,1]{1,0:T(1,128)} %get-tuple-element.9.count_ref), custom_call_target="tpu_custom_call" | custom-call | tf_op jit(solution)/shard_map/unpack/pallas_call | solution.py:385

commit v4 on v3

--- a/solution.py
+++ b/solution.py
@@ -19,6 +19,8 @@
 PREV = {Y: X, Z: Y, X: Z}
 XYZ = X + Y + Z
 LOSS_LANE = 64
+HID_PIECES = ((0, 88), (88, 88), (176, 80))
+TURN = {X: (0, 1, 2), Y: (1, 0, 2), Z: (0, 1, 2)}
 
 ORDER = [(0, 0), (0, 1)]
 for group in ((X, Y, Z), (X + Y, Y + Z, Z + X), (XYZ,)):
@@ -29,7 +31,7 @@
 AG_X, AG_Y = 0, AG_COPIES
 RS_D2, RS_D1 = 2 * AG_COPIES, 2 * AG_COPIES + RS_COPIES
 AR = 2 * AG_COPIES + 2 * RS_COPIES
-N_SEM = AR + 60
+N_SEM = AR + 120
 
 
 def peer(me, mask):
@@ -41,9 +43,9 @@
 
 
 def kernel(a_hbm, x_hbm, wh_ref, wo_ref, lab_ref, tm_ref,
-           sums_ref, count_ref,
+           osums_ref, hsums_ref, count_ref,
            a_v, xg, yg, y1, z1, hid, pos, z2, r2, ra2, rb2, rc2, r1, ra1, rb1, rc1, stage, wop,
-           fsrc, frecv, fsum, fall, a_sem, x_sem, send_sem, recv_sem):
+           osrc, orecv, osum, oall, hsrc, hrecv, hsum, hall, a_sem, x_sem, send_sem, recv_sem):
     me = lax.axis_index(AXIS)
     devs = {m: peer(me, m) for m in range(16)}
 
@@ -120,6 +122,7 @@
             a_copies[s].start()
         if part == 0:
             z1[...] = jnp.zeros_like(z1)
+            hsrc[...] = jnp.zeros_like(hsrc)
 
     def layer_one(lo, hi):
         for s in range(lo, hi):
@@ -174,7 +177,7 @@
     grad = (jnp.exp(zt - lse) - hot.astype(F32)) * (tm / total)
     gt = jnp.where(valid, grad, 0.0).astype(BF16)
 
-    def scatter(base, r, ra, rb, rc, pieces, left, stages, early, middle, late):
+    def scatter(base, r, ra, rb, rc, pieces, left, stages, early, middle, late, final):
         def rows(i):
             return pl.ds(*pieces[i])
 
@@ -229,9 +232,10 @@
         for k, d in enumerate(DIMS):
             q = d + NEXT[d]
             produce(1 + k)
-            for i, e in enumerate(DIMS):
-                if e + q != XYZ:
-                    two[d, i] = send(q, i, rb.at[k, rows(i)], base + 11 + 3 * k + i, d)
+            for i in TURN[d]:
+                if DIMS[i] + q == XYZ:
+                    break
+                two[d, i] = send(q, i, rb.at[k, rows(i)], base + 11 + 3 * k + i, d)
 
         def outer():
             for i, e in enumerate(DIMS):
@@ -240,15 +244,15 @@
                 r[q, rows(i)] = r[q, rows(i)] + ra[rows(i)]
                 d = NEXT[e]
                 k = DIMS.index(d)
-                two[d, i] = send(q, i, rb.at[k, rows(i)], base + 11 + 3 * k + i, d)
+                for n in TURN[d][TURN[d].index(i):]:
+                    two[d, n] = send(q, n, rb.at[k, rows(n)], base + 11 + 3 * k + n, d)
 
         def inner():
             for j in range(3):
                 for n, e in enumerate(DIMS):
                     d = PREV[e]
                     k = DIMS.index(d)
-                    last = DIMS.index(XYZ - d - NEXT[d])
-                    i = (last + 1 + j) % 3
+                    i = TURN[d][j]
                     two[d, i].wait_recv()
                     r[e, rows(i)] = r[e, rows(i)] + rb[k, rows(i)]
                     one[e, i] = send(e, i, rc.at[n, rows(i)], base + 20 + 3 * n + i, e)
@@ -257,25 +261,28 @@
             outer()
         for k, d in enumerate(DIMS):
             produce(4 + k)
+            if k == 1 and not early:
+                outer()
         if early:
             inner()
             produce(7)
         else:
             produce(7)
             middle()
-            outer()
             inner()
         late()
         for j in range(3):
             for n, e in enumerate(DIMS):
-                i = (DIMS.index(XYZ - PREV[e] - e) + 1 + j) % 3
+                i = TURN[PREV[e]][j]
                 one[e, i].wait_recv()
                 r[0, rows(i)] = r[0, rows(i)] + rc[n, rows(i)]
+            for i in ((), (0, 1), (2,))[j]:
+                final(i)
 
     def stage_d2(k):
         return stage.at[k // 4, pl.ds(CP * (k % 4), CP)]
 
-    scatter(RS_D2, r2, ra2, rb2, rc2, ((0, 16), (16, 16), (32, 16)), gt, stage_d2, True, None, lambda: None)
+    scatter(RS_D2, r2, ra2, rb2, rc2, ((0, 16), (16, 16), (32, 16)), gt, stage_d2, True, None, lambda: None, lambda i: None)
 
     d2t = r2[0].astype(BF16)
     for cp in sent:
@@ -285,26 +292,37 @@
     pos[...] = jnp.where(pos[...] > 0, grad_hid, 0.0).astype(BF16)
 
     parts = {}
+    bufs = [(osrc, orecv, osum, oall)] + [(hsrc.at[i], hrecv.at[i], hsum.at[i], hall.at[i]) for i in range(3)]
 
     def exchange(n, values):
-        for i in range(NB):
-            fsrc[n, i] = values[16 * i:16 * i + 16]
+        src, recv, _, _ = bufs[n]
+        per = -(-values.shape[0] // NB)
+        for i in range(0, NB):
+            rows = values[per * i:per * i + per]
+            if rows.shape[0]:
+                src[i, 0:rows.shape[0], 0:rows.shape[1]] = rows
         k = AR + 30 * n - 1
-        parts[n] = [start(rcopy(fsrc.at[n, devs[m]], frecv.at[n, m], k + m, m)) for m in range(1, 16)]
+        parts[n] = [start(rcopy(src.at[devs[m]], recv.at[m], k + m, m)) for m in range(1, 16)]
 
     def share(n):
-        acc = fsrc[n, me]
+        src, recv, total_n, out = bufs[n]
+        acc = src[me]
         for m in range(1, 16):
             parts[n][m - 1].wait_recv()
-            acc = acc + frecv[n, m]
-        fsum[n] = acc
-        fall[n, me] = acc
+            acc = acc + recv[m]
+        total_n[...] = acc
+        out[me] = acc
         for m in range(1, 16):
-            start(rcopy(fsum.at[n], fall.at[n, me], AR + 30 * n + 14 + m, m))
+            start(rcopy(total_n, out.at[me], AR + 30 * n + 14 + m, m))
 
     def collect(n):
+        _, _, total_n, out = bufs[n]
         for m in range(1, 16):
-            rcopy(fsum.at[n], fall.at[n, devs[m]], AR + 30 * n + 14 + m, m).wait_recv()
+            rcopy(total_n, out.at[devs[m]], AR + 30 * n + 14 + m, m).wait_recv()
+
+    def hidden_grad(i):
+        d1t = r1[0, pl.ds(*HID_PIECES[i])].astype(BF16)
+        exchange(1 + i, lax.dot_general(d1t, xg[0], LAST, preferred_element_type=F32))
 
     def middle():
         gwo_t = jnp.dot(d2t, hid[...], preferred_element_type=F32)
@@ -315,24 +333,26 @@
     def stage_d1(k):
         return stage.at[k % 2]
 
-    scatter(RS_D1, r1, ra1, rb1, rc1, ((0, 88), (88, 88), (176, 80)), pos, stage_d1, False, middle, lambda: share(0))
-
-    d1t = r1[0].astype(BF16)
-    gwh_t = lax.dot_general(d1t, xg[0], LAST, preferred_element_type=F32)
-    exchange(1, jnp.concatenate([gwh_t, jnp.zeros((HID, 128 - FI), F32)], axis=1))
-    share(1)
-    collect(0)
-    collect(1)
-    for n in range(2):
-        for i in range(NB):
-            sums_ref[n, i] = fall[n, i]
+    scatter(RS_D1, r1, ra1, rb1, rc1, HID_PIECES, pos, stage_d1, False, middle, lambda: share(0), hidden_grad)
+
+    for n in range(1, 4):
+        share(n)
+    for n in range(4):
+        collect(n)
+    osums_ref[...] = oall[...]
+    hsums_ref[...] = hall[...]
     count_ref[...] = total
     for cp in sent:
         cp.wait_send()
 
 
-def unpack(sums_ref, count_ref, loss_ref, gwh_ref, gwo_ref):
-    gwo, gwh = (jnp.concatenate([sums_ref[n, i] for i in range(NB)], axis=0) for n in range(2))
+def unpack(osums_ref, hsums_ref, count_ref, loss_ref, gwh_ref, gwo_ref, rows_ref):
+    gwo = jnp.concatenate([osums_ref[i] for i in range(NB)], axis=0)
+    for p, (lo, size) in enumerate(HID_PIECES):
+        per = -(-size // NB)
+        for i in range(NB):
+            rows_ref[lo + per * i:lo + per * i + per] = hsums_ref[p, i, 0:per]
+    gwh = rows_ref[0:HID]
     gwh_ref[...] = jnp.transpose(gwh)[:FI]
     gwo_ref[...] = jnp.transpose(gwo)[:NC]
     loss_ref[...] = gwo[0:1, LOSS_LANE:LOSS_LANE + 1] / count_ref[...]
@@ -342,14 +362,15 @@
     del block_mask
     vmem = pl.BlockSpec(memory_space=pltpu.VMEM)
     hbm = pl.BlockSpec(memory_space=pl.ANY)
-    sums, count = pl.pallas_call(
+    osums, hsums, count = pl.pallas_call(
         kernel,
         out_shape=(
-            jax.ShapeDtypeStruct((2, NB, 16, 128), F32),
+            jax.ShapeDtypeStruct((NB, 16, 128), F32),
+            jax.ShapeDtypeStruct((3, NB, 8, 128), F32),
             jax.ShapeDtypeStruct((1, 1), F32),
         ),
         in_specs=[hbm, hbm, vmem, vmem, vmem, vmem],
-        out_specs=(vmem, vmem),
+        out_specs=(vmem, vmem, vmem),
         scratch_shapes=[
             pltpu.VMEM((NB, BR, BR), BF16),
             pltpu.VMEM((NB, FI, BR), BF16),
@@ -369,10 +390,14 @@
             pltpu.VMEM((3, HID, BR), F32),
             pltpu.VMEM((2, HID, BR), F32),
             pltpu.VMEM((CP, HID), BF16),
-            pltpu.VMEM((2, NB, 16, 128), F32),
-            pltpu.VMEM((2, NB, 16, 128), F32),
-            pltpu.VMEM((2, 16, 128), F32),
-            pltpu.VMEM((2, NB, 16, 128), F32),
+            pltpu.VMEM((NB, 16, 128), F32),
+            pltpu.VMEM((NB, 16, 128), F32),
+            pltpu.VMEM((16, 128), F32),
+            pltpu.VMEM((NB, 16, 128), F32),
+            pltpu.VMEM((3, NB, 8, 128), F32),
+            pltpu.VMEM((3, NB, 8, 128), F32),
+            pltpu.VMEM((3, 8, 128), F32),
+            pltpu.VMEM((3, NB, 8, 128), F32),
             pltpu.SemaphoreType.DMA((NB,)),
             pltpu.SemaphoreType.DMA,
             pltpu.SemaphoreType.DMA((N_SEM,)),
@@ -389,10 +414,11 @@
             jax.ShapeDtypeStruct((FI, HID), F32),
             jax.ShapeDtypeStruct((NC, HID), F32),
         ),
-        in_specs=[vmem, vmem],
+        in_specs=[vmem, vmem, vmem],
         out_specs=(vmem, vmem, vmem),
+        scratch_shapes=[pltpu.VMEM((HID + 16, 128), F32)],
         name='unpack',
-    )(sums, count)
+    )(osums, hsums, count)
     return loss[0, 0], gwh, gwo.T
 
 

time: 133 us -> 134 us (level)
  no operation moved by 1% of the time
where the time goes in v4:
time: 134 us
  Pallas kernels  134 us (100%)
    pallas_call x1, Pallas kernels, device_step(): pl.pallas_call(kernel, out_shape=(jax.ShapeDtypeStruct((NB, 16, 128), F32...  131 us

profile of v4, /device:TPU:0, one launch (start us, length us, event | category | flops | bytes accessed | tf_op | source)
XLA Modules:
  0.0 134.2 jit_solution(8397241352184633437)
XLA Ops:
  0.6 131.1 %gcn_step.1 = (f32[16,16,128]{2,1,0:T(8,128)}, f32[3,16,8,128]{3,2,1,0:T(8,128)}, f32[1,1]{1,0:T(1,128)}) custom-call(bf16[1024,16384]{1,0:T(8,128)(2,1)} %a_hbm.1, bf16[100,1024]{1,0:T(8,128)(2,1)} %bitcast.6, f32[100,256]{1,0:T(8,128)} %wh_ref.1, f32[47,256]{1,0:T(8,128)} %bitcast.7, s32[1,1024]{1,0:T(1,128)} %bitcast.8, s32[1,1024]{1,0:T(1,128)} %bitcast.9), custom_call_target="tpu_custom_call" | custom-call | tf_op jit(solution)/shard_map/gcn_step/pallas_call | solution.py:365
  131.8 2.4 %unpack.1 = (f32[1,1]{1,0:T(1,128)}, f32[100,256]{1,0:T(8,128)}, f32[47,256]{1,0:T(8,128)}) custom-call(f32[16,16,128]{2,1,0:T(8,128)} %get-tuple-element.9.osums_ref, f32[3,16,8,128]{3,2,1,0:T(8,128)} %get-tuple-element.10.hsums_ref, f32[1,1]{1,0:T(1,128)} %get-tuple-element.11.count_ref), custom_call_target="tpu_custom_call" | custom-call | tf_op jit(solution)/shard_map/unpack/pallas_call | solution.py:410

commit v5 on v3

--- a/solution.py
+++ b/solution.py
@@ -20,12 +20,12 @@
 XYZ = X + Y + Z
 LOSS_LANE = 64
 
-ORDER = [(0, 0), (0, 1)]
-for group in ((X, Y, Z), (X + Y, Y + Z, Z + X), (XYZ,)):
-    ORDER += [(q, 0) for q in group] + [(q, 1) for q in group]
+PLACES = (0, X, Y, Z, X + Y, Y + Z, Z + X, XYZ)
+PLACE = {q: j for j, q in enumerate(PLACES)}
+ORDER = [(q, c) for q in PLACES for c in (0, 1)]
 SLOT = {qc: i for i, qc in enumerate(ORDER)}
 
-AG_COPIES, RS_COPIES = 17, 29
+AG_COPIES, RS_COPIES = 17, 31
 AG_X, AG_Y = 0, AG_COPIES
 RS_D2, RS_D1 = 2 * AG_COPIES, 2 * AG_COPIES + RS_COPIES
 AR = 2 * AG_COPIES + 2 * RS_COPIES
@@ -76,6 +76,53 @@
         return cp
 
     def gather(base, g, pieces, work, load):
+        one, two, three = {}, {}, {}
+        half = {q: rcopy(g.at[SLOT[q, 0]], g.at[SLOT[q, 1]], base + 9 + q, 1) for q in PLACES}
+        for i, d in enumerate(DIMS):
+            e, rows = NEXT[d], pl.ds(*pieces[i])
+            one[d] = rcopy(g.at[0], g.at[SLOT[d, 0]], base + i, 2 * d)
+            two[d] = rcopy(g.at[SLOT[e, 0]], g.at[SLOT[d + e, 0]], base + 3 + i, 2 * d)
+            three[d] = rcopy(g.at[SLOT[XYZ - d, 0], rows], g.at[SLOT[XYZ, 0], rows], base + 6 + i, 2 * d)
+        for d in DIMS:
+            start(one[d])
+        start(half[0])
+        load(0)
+
+        def second():
+            for d in DIMS:
+                one[NEXT[d]].wait_recv()
+                start(two[d])
+            for d in DIMS:
+                start(half[d])
+            load(1)
+
+        def third():
+            for d in DIMS:
+                two[NEXT[d]].wait_recv()
+                start(three[d])
+            for d in DIMS:
+                start(half[XYZ - d])
+            half[Z].wait_recv()
+
+        def fourth():
+            for d in DIMS:
+                three[d].wait_recv()
+            start(half[XYZ])
+            half[Y + Z].wait_recv()
+
+        events = {2: second, 7: third, 11: fourth}
+        for q in PLACES:
+            events.setdefault(SLOT[q, 1], half[q].wait_recv)
+
+        def step(n, carry):
+            for at, event in events.items():
+                pl.when(n == at)(event)
+            work(n)
+            return carry
+
+        lax.fori_loop(0, NB, step, 0)
+
+    def gather_straight(base, g, pieces, work, load):
         def core_fwd(q):
             return start(rcopy(g.at[SLOT[q, 0]], g.at[SLOT[q, 1]], base + 9 + q, 1))
 
@@ -83,9 +130,9 @@
         half = {0: core_fwd(0)}
         two, three = {}, {}
         load(0)
-        work(0, 1)
+        work([0])
         half[0].wait_recv()
-        work(1, 2)
+        work([1])
         for i, d in enumerate(DIMS):
             e = NEXT[d]
             one[e].wait_recv()
@@ -93,25 +140,26 @@
         for d in DIMS:
             half[d] = core_fwd(d)
         load(1)
-        work(2, 5)
+        work([2, 4, 6])
         for d in DIMS:
             half[d].wait_recv()
-        work(5, 8)
+        work([3, 5])
         for i, d in enumerate(DIMS):
             rows = pl.ds(*pieces[i])
             two[NEXT[d]].wait_recv()
             three[d] = start(rcopy(g.at[SLOT[XYZ - d, 0], rows], g.at[SLOT[XYZ, 0], rows], base + 6 + i, 2 * d))
         for d in DIMS:
             half[XYZ - d] = core_fwd(XYZ - d)
-        work(8, 11)
+        work([7, 8, 10])
+        work([12])
         for d in DIMS:
             three[d].wait_recv()
         half[XYZ] = core_fwd(XYZ)
         for d in DIMS:
             half[XYZ - d].wait_recv()
-        work(11, 14)
+        work([9, 11, 13])
         half[XYZ].wait_recv()
-        work(14, 16)
+        work([14, 15])
 
     wh = wh_ref[...].astype(BF16)
 
@@ -121,20 +169,16 @@
         if part == 0:
             z1[...] = jnp.zeros_like(z1)
 
-    def layer_one(lo, hi):
-        for s in range(lo, hi):
+    def layer_one(slots):
+        bufs = (hid, y1.at[0], y1.at[1])
+        for s in slots:
             a_copies[s].wait()
-
-        def proj(s, ref):
-            ref[...] = lax.dot_general(xg[s], wh, FIRST, preferred_element_type=F32).astype(BF16)
-
-        bufs = (hid, y1.at[0], y1.at[1])
-        for n, s in enumerate(range(lo, hi)):
-            proj(s, bufs[n])
-        for n, s in enumerate(range(lo, hi)):
+        for n, s in enumerate(slots):
+            bufs[n][...] = lax.dot_general(xg[s], wh, FIRST, preferred_element_type=F32).astype(BF16)
+        for n, s in enumerate(slots):
             z1[...] += jnp.dot(a_v[s], bufs[n][...], preferred_element_type=F32)
 
-    gather(AG_X, xg, ((0, 32), (32, 32), (64, 36)), layer_one, load_a)
+    gather_straight(AG_X, xg, ((0, 32), (32, 32), (64, 36)), layer_one, load_a)
 
     hid[...] = jnp.maximum(z1[...], 0.0).astype(BF16)
     tm = tm_ref[...].astype(F32)
@@ -142,23 +186,14 @@
     row = lax.broadcasted_iota(jnp.int32, (CP, BR), 0)
     yg[0] = jnp.where(row == NC, tm, y2t).astype(BF16)
 
-    first = [True]
-
-    def layer_two(lo, hi):
-        def body(s, carry):
-            z2[:, :CP] += lax.dot_general(a_v[s], yg[s], LAST, preferred_element_type=F32)
-            return carry
-
-        if 2 <= lo < 8:
-            lax.fori_loop(lo, hi, body, 0)
-        else:
-            for s in range(lo, hi):
-                body(s, 0)
-        if first[0]:
-            first[0] = False
+    def layer_two(n):
+        z2[:, :CP] += lax.dot_general(a_v[n], yg[n], LAST, preferred_element_type=F32)
+
+    def keep_sign(part):
+        if part == 0:
             pos[...] = jnp.where(jnp.transpose(z1[...]) > 0, 1.0, 0.0).astype(BF16)
 
-    gather(AG_Y, yg, ((0, 16), (16, 16), (32, 16)), layer_two, lambda part: None)
+    gather(AG_Y, yg, ((0, 16), (16, 16), (32, 16)), layer_two, keep_sign)
 
     count = jnp.zeros((1, BR), F32)
     for s in range(NB):
@@ -174,94 +209,102 @@
     grad = (jnp.exp(zt - lse) - hot.astype(F32)) * (tm / total)
     gt = jnp.where(valid, grad, 0.0).astype(BF16)
 
-    def scatter(base, r, ra, rb, rc, pieces, left, stages, early, middle, late):
+    def scatter(base, r, ra, rb, rc, pieces, left, early, middle, late):
         def rows(i):
             return pl.ds(*pieces[i])
 
-        pair = {}
-
-        def other(k, q):
-            st = stages(k)
-            if not early and k >= 2:
-                pair[k - 2].wait_send()
-                sent[:] = [cp for cp in sent if cp is not pair[k - 2]]
-            if early or k == 0:
-                st[...] = jnp.dot(left[...], a_v[SLOT[q, 1]], preferred_element_type=F32)
+        def pair(k):
+            return rcopy(stage.at[k % 2, pl.ds(0, left.shape[0])], r.at[7 - k], base + k, 1)
+
+        def other(k):
+            pl.when(k >= (2 if early else 3))(lambda: pair(k - 2).wait_send())
+            stage[k % 2, 0:left.shape[0]] = jnp.dot(left[...], a_v[15 - 2 * k], preferred_element_type=F32)
+            pair(k).start()
+
+        def own(k):
+            if early:
+                mine = jnp.dot(left[...], a_v[14 - 2 * k], preferred_element_type=F32)
+                pair(k).wait_recv()
+                r[7 - k] = r[7 - k] + mine
             else:
-                def body(h, carry):
-                    cols = pl.ds(pl.multiple_of(h * 512, 512), 512)
-                    st[:, cols] = jnp.dot(left[...], a_v[SLOT[q, 1], :, cols], preferred_element_type=F32)
-                    return carry
-
-                lax.fori_loop(0, 2, body, 0)
-            pair[k] = start(rcopy(st, r.at[q], base + k, 1))
-
-        def own(k, q):
-            if early:
-                mine = jnp.dot(left[...], a_v[SLOT[q, 0]], preferred_element_type=F32)
-                pair[k].wait_recv()
-                r[q] = r[q] + mine
-            else:
-                pair[k].wait_recv()
-
-                def body(h, carry):
-                    cols = pl.ds(pl.multiple_of(h * 512, 512), 512)
-                    r[q, :, cols] = r[q, :, cols] + jnp.dot(left[...], a_v[SLOT[q, 0], :, cols], preferred_element_type=F32)
-                    return carry
-
-                lax.fori_loop(0, 2, body, 0)
+                pair(k).wait_recv()
+                r[7 - k] = r[7 - k] + jnp.dot(left[...], a_v[14 - 2 * k], preferred_element_type=F32)
 
         def send(q, i, dst, k, d):
-            return start(rcopy(r.at[q, rows(i)], dst, k, 2 * d))
+            return rcopy(r.at[PLACE[q], rows(i)], dst, k, 2 * d)
 
         three, two, one = {}, {}, {}
-        order = (XYZ,) + tuple(d + NEXT[d] for d in DIMS) + DIMS + (0,)
-
-        def produce(k):
-            if k < 7:
-                other(k + 1, order[k + 1])
-            own(k, order[k])
-
-        other(0, XYZ)
-        produce(0)
-        for i, d in enumerate(DIMS):
-            three[d] = send(XYZ, i, ra.at[rows(i)], base + 8 + i, d)
         for k, d in enumerate(DIMS):
             q = d + NEXT[d]
-            produce(1 + k)
+            three[d] = send(XYZ, k, ra.at[rows(k)], base + 8 + k, d)
+            for i in range(3):
+                two[d, i] = send(q, i, rb.at[k, rows(i)], base + 11 + 3 * k + i, d)
+                one[d, i] = send(d, i, rc.at[k, rows(i)], base + 20 + 3 * k + i, d)
+
+        def corner():
+            for d in DIMS:
+                start(three[d])
+
+        def edge(d):
             for i, e in enumerate(DIMS):
-                if e + q != XYZ:
-                    two[d, i] = send(q, i, rb.at[k, rows(i)], base + 11 + 3 * k + i, d)
+                if e + d + NEXT[d] != XYZ:
+                    start(two[d, i])
 
         def outer():
             for i, e in enumerate(DIMS):
                 three[e].wait_recv()
-                q = XYZ - e
-                r[q, rows(i)] = r[q, rows(i)] + ra[rows(i)]
-                d = NEXT[e]
-                k = DIMS.index(d)
-                two[d, i] = send(q, i, rb.at[k, rows(i)], base + 11 + 3 * k + i, d)
+                j = PLACE[XYZ - e]
+                r[j, rows(i)] = r[j, rows(i)] + ra[rows(i)]
+                start(two[NEXT[e], i])
 
         def inner():
             for j in range(3):
-                for n, e in enumerate(DIMS):
+                for e in DIMS:
                     d = PREV[e]
                     k = DIMS.index(d)
-                    last = DIMS.index(XYZ - d - NEXT[d])
-                    i = (last + 1 + j) % 3
+                    i = (DIMS.index(XYZ - d - e) + 1 + j) % 3
                     two[d, i].wait_recv()
-                    r[e, rows(i)] = r[e, rows(i)] + rb[k, rows(i)]
-                    one[e, i] = send(e, i, rc.at[n, rows(i)], base + 20 + 3 * n + i, e)
-
+                    r[PLACE[e], rows(i)] = r[PLACE[e], rows(i)] + rb[k, rows(i)]
+                    start(one[e, i])
+
+        def edges():
+            edge(X)
+            if early:
+                outer()
+
+        events = {1: corner, 2: lambda: edge(Z), 3: lambda: edge(Y), 4: edges}
         if early:
-            outer()
-        for k, d in enumerate(DIMS):
-            produce(4 + k)
+            events[7] = inner
+
+        def step(k, carry):
+            pl.when(k < 8)(lambda: other(k))
+            pl.when(k >= 1)(lambda: own(k - 1))
+            for at, event in events.items():
+                pl.when(k == at)(event)
+            return carry
+
         if early:
-            inner()
-            produce(7)
+            lax.fori_loop(0, 9, step, 0)
         else:
-            produce(7)
+            stage[0] = jnp.dot(left[...], a_v[15], preferred_element_type=F32)
+            thirds = [
+                rcopy(stage.at[0, rows(i)], r.at[7, rows(i)], base + (0, 29, 30)[i], 1) for i in range(3)]
+            for cp in thirds:
+                cp.start()
+            stage[1] = jnp.dot(left[...], a_v[14], preferred_element_type=F32)
+            for i, d in enumerate(DIMS):
+                thirds[i].wait_recv()
+                r[7, rows(i)] = r[7, rows(i)] + stage[1, rows(i)]
+                start(three[d])
+            stage[1] = jnp.dot(left[...], a_v[13], preferred_element_type=F32)
+            pair(1).start()
+            for cp in thirds:
+                cp.wait_send()
+            events.pop(1)
+            lax.fori_loop(2, 9, step, 0)
+        for k in (6, 7):
+            pair(k).wait_send()
+        if not early:
             middle()
             outer()
             inner()
@@ -272,10 +315,7 @@
                 one[e, i].wait_recv()
                 r[0, rows(i)] = r[0, rows(i)] + rc[n, rows(i)]
 
-    def stage_d2(k):
-        return stage.at[k // 4, pl.ds(CP * (k % 4), CP)]
-
-    scatter(RS_D2, r2, ra2, rb2, rc2, ((0, 16), (16, 16), (32, 16)), gt, stage_d2, True, None, lambda: None)
+    scatter(RS_D2, r2, ra2, rb2, rc2, ((0, 16), (16, 16), (32, 16)), gt, True, None, lambda: None)
 
     d2t = r2[0].astype(BF16)
     for cp in sent:
@@ -312,10 +352,7 @@
         lane = lax.broadcasted_iota(jnp.int32, (HID, 128), 1)
         exchange(0, jnp.where(lane == LOSS_LANE, loss, gwo))
 
-    def stage_d1(k):
-        return stage.at[k % 2]
-
-    scatter(RS_D1, r1, ra1, rb1, rc1, ((0, 88), (88, 88), (176, 80)), pos, stage_d1, False, middle, lambda: share(0))
+    scatter(RS_D1, r1, ra1, rb1, rc1, ((0, 88), (88, 88), (176, 80)), pos, False, middle, lambda: share(0))
 
     d1t = r1[0].astype(BF16)
     gwh_t = lax.dot_general(d1t, xg[0], LAST, preferred_element_type=F32)

time: 133 us -> 133 us (level)
  no operation moved by 1% of the time
where the time goes in v5:
time: 133 us
  Pallas kernels  132 us (99%)
    pallas_call x1, Pallas kernels, device_step(): pl.pallas_call(kernel, out_shape=(jax.ShapeDtypeStruct((2, NB, 16, 128),...  130 us

profile of v5, /device:TPU:0, one launch (start us, length us, event | category | flops | bytes accessed | tf_op | source)
XLA Modules:
  0.0 133.1 jit_solution(11550537929365824432)
XLA Ops:
  0.6 130.2 %gcn_step.1 = (f32[2,16,16,128]{3,2,1,0:T(8,128)}, f32[1,1]{1,0:T(1,128)}) custom-call(bf16[1024,16384]{1,0:T(8,128)(2,1)} %a_hbm.1, bf16[100,1024]{1,0:T(8,128)(2,1)} %bitcast.6, f32[100,256]{1,0:T(8,128)} %wh_ref.1, f32[47,256]{1,0:T(8,128)} %bitcast.7, s32[1,1024]{1,0:T(1,128)} %bitcast.8, s32[1,1024]{1,0:T(1,128)} %bitcast.9), custom_call_target="tpu_custom_call" | custom-call | tf_op jit(solution)/shard_map/gcn_step/pallas_call | solution.py:382
  130.8 2.3 %unpack.1 = (f32[1,1]{1,0:T(1,128)}, f32[100,256]{1,0:T(8,128)}, f32[47,256]{1,0:T(8,128)}) custom-call(f32[2,16,16,128]{3,2,1,0:T(8,128)} %get-tuple-element.8.sums_ref, f32[1,1]{1,0:T(1,128)} %get-tuple-element.9.count_ref), custom_call_target="tpu_custom_call" | custom-call | tf_op jit(solution)/shard_map/unpack/pallas_call | solution.py:422
